TPU v7x, 32 devices: a whole 2x2x4 slice. The times are simulated.
32 devices in a mesh: grp: 2 (over y), freq: 4 (over z), beam: 2 (over x), dm: 2 (over core).
Axes of the slice: x: 2, y: 2, z: 4, core: 2. Of those that a mesh axis runs over, the one named last changes fastest.
Arguments:
- voltages: bfloat16 [4, 2048, 16, 2, 1024], P(None, ('freq', 'beam'), ('grp', 'dm')), parts along dimension 2, may hold values from -6 to 6
- grid_feed: int32 [1024], replicated, may hold values from 0 to 1023, each once
- delays: int32 [4, 2048, 256], P('freq', None, 'dm'), may hold values from 0 to 4
Outputs:
- dedispersed: float32 [4, 256, 8, 1024], P('freq', 'dm', 'grp', 'beam'), parts along dimension 2
There are 2 independent parts, one for each index of `grp`. A program takes and returns all parts, laid end to end along the dimension named above; an argument that names none is the same for every part. Nothing has to cross between parts.
Inputs may be any that keep to these rules, and one draw needn't show every extreme that they name: `grid_feed`: each feed appears once.
All inputs are finite; a program needn't handle non-finite values.
Results may differ from a plain program's by a relative error of at most 0.0034.
Values may be sent and summed in bfloat16 or wider, within the bound.
A program may use at most 128 MiB of HBM per device.

v0:
```python
import functools
import math

import jax
import jax.numpy as jnp
import numpy as np
from jax import lax
from jax.experimental import pallas as pl
from jax.experimental.pallas import tpu as pltpu
from jax.sharding import PartitionSpec as P

GX = 4
GY = 256
FREQS = 8192
ROWS = 16
LAGS = 5
BEHIND = 5
MESH = pl.DeviceIdType.MESH


def steering_table(length, factor):
    position = jnp.arange(length, dtype=jnp.int32)
    phase_step = position[:, None] * position[None, :] % length
    phase_angle = phase_step.astype(jnp.float32) * (2.0 * math.pi / length)
    cosine = jnp.cos(phase_angle) * factor
    sine_part = jnp.sin(phase_angle) * factor
    upper_half = jnp.concatenate([cosine, -sine_part], axis=1)
    lower_half = jnp.concatenate([sine_part, cosine], axis=1)
    return jnp.concatenate([upper_half, lower_half], axis=0).astype(jnp.bfloat16)


def quarter_table():
    position = jnp.arange(GX, dtype=jnp.int32)
    phase_step = position[:, None] * position[None, :] % GX
    cosine = jnp.where(phase_step == 0, 1.0, jnp.where(phase_step == 2, -1.0, 0.0)) * 0.5
    sine_part = jnp.where(phase_step == 1, 1.0, jnp.where(phase_step == 3, -1.0, 0.0)) * 0.5
    real_in = jnp.stack([cosine, -sine_part], axis=2)
    imag_in = jnp.stack([sine_part, cosine], axis=2)
    return jnp.stack([real_in, imag_in], axis=1).astype(jnp.float32)


def form_power(voltages, grid_feed):
    row_count = voltages.shape[0] * voltages.shape[1] * voltages.shape[2]
    feed_count = voltages.shape[4]
    gridded = jnp.take(voltages.reshape(row_count, 2, feed_count), grid_feed, axis=2)
    gridded = jnp.transpose(gridded.reshape(row_count, 2, GX, GY), (0, 2, 1, 3)).reshape(
        row_count * GX, 2 * GY
    )
    along_y = jnp.dot(
        gridded, steering_table(GY, 1.0 / math.sqrt(GY)), preferred_element_type=jnp.float32
    ).astype(jnp.bfloat16)
    along_y = along_y.reshape(row_count, GX, 2, GY).astype(jnp.float32)
    formed = jnp.einsum(
        "rgpy,gpbq->rbqy", along_y, quarter_table(), precision=lax.Precision.HIGHEST
    )
    intensity = 0.5 * (formed[:, :, 0, :] ** 2 + formed[:, :, 1, :] ** 2)
    return intensity.astype(jnp.bfloat16).reshape(row_count, feed_count)


def regrouped_body(voltages, grid_feed, delays):
    band_count, sub_local, time_local = (voltages.shape[0], voltages.shape[1], voltages.shape[2])
    feed_count = voltages.shape[4]
    columns = lax.axis_size("beam")
    col_width = feed_count // columns
    intensity = form_power(voltages, grid_feed).reshape(
        band_count, sub_local, time_local, columns, col_width
    )
    regrouped = jnp.transpose(intensity, (0, 3, 1, 2, 4)).reshape(
        band_count * columns, sub_local, time_local, col_width
    )
    turned = lax.all_to_all(regrouped, ("freq", "beam"), split_axis=0, concat_axis=1, tiled=True)
    turned = turned.reshape(-1, time_local, col_width)
    full_time = lax.all_gather(turned, "dm", axis=1, tiled=True)
    sub_count, total_time = (full_time.shape[0], full_time.shape[1])
    levels = full_time.astype(jnp.float32)
    centered = (levels - jnp.mean(levels, axis=1, keepdims=True)).astype(jnp.bfloat16)
    flattened = centered.reshape(sub_count * total_time, col_width)
    out_time = total_time // 2
    offsets = jnp.arange(out_time, dtype=jnp.int32)
    sample_ids = jnp.arange(total_time, dtype=jnp.int32)
    dm_local = delays.shape[2]
    dm_block = 32
    lag_blocks = jnp.transpose(delays[0]).reshape(dm_local // dm_block, dm_block, sub_count)

    def dedisperse(lag_rows):
        shifted = offsets[None, :, None] + lag_rows[:, None, :]
        selector = (shifted[:, :, :, None] == sample_ids[None, None, None, :]).astype(jnp.bfloat16)
        summed = jnp.dot(
            selector.reshape(dm_block * out_time, sub_count * total_time),
            flattened,
            preferred_element_type=jnp.float32,
        )
        return summed.reshape(dm_block, out_time, col_width)

    partial_sum = lax.map(dedisperse, lag_blocks).reshape(dm_local, out_time, col_width)
    cumulative = lax.all_to_all(
        jnp.cumsum(
            lax.all_to_all(partial_sum[None], "freq", split_axis=1, concat_axis=0, tiled=True),
            axis=0,
        ),
        "freq",
        split_axis=0,
        concat_axis=1,
        tiled=True,
    )
    return cumulative * (1.0 / math.sqrt(FREQS))


def half_table():
    half = GY // 2
    cell = np.arange(GY)
    row = np.arange(half)
    angle = (cell[:, None] * row[None, :] % GY).astype(np.float32) * np.float32(2.0 * math.pi / GY)
    factor = np.float32(1.0 / math.sqrt(GY))
    sines = np.sin(angle) * factor
    sines[:, 0] = np.where(cell % 2 == 0, 1.0, -1.0) * factor
    table = np.concatenate([np.cos(angle) * factor, sines], axis=1)
    return jnp.asarray(table.astype(jnp.bfloat16))


def place_table(feed_ref, table_ref, full_ref):
    feeds = full_ref.shape[0]
    feed = lax.broadcasted_iota(jnp.int32, (feeds, GY), 0)
    for g in range(GX):
        cells = slice(g * GY, (g + 1) * GY)
        placed = jnp.where(feed == feed_ref[:, cells], 1.0, 0.0).astype(jnp.bfloat16)
        full_ref[:, cells] = jnp.dot(
            placed, table_ref[...], preferred_element_type=jnp.float32
        ).astype(jnp.bfloat16)


def beamform(volt_ref, full_ref, line_ref, level_ref):
    channels, feeds = volt_ref.shape[1], volt_ref.shape[4]
    half = GY // 2
    pairs = volt_ref[0, :, 0].reshape(2 * channels, feeds)
    for g in range(GX):
        line = jnp.dot(
            pairs, full_ref[:, g * GY : (g + 1) * GY], preferred_element_type=jnp.float32
        )
        line_ref[2 * g], line_ref[2 * g + 1] = line[:, :half], line[:, half:]
    first = lax.broadcasted_iota(jnp.int32, (ROWS, half), 1) == 0

    def rounded(a):
        return a.astype(jnp.bfloat16).astype(jnp.float32)

    for row in range(0, channels, ROWS):
        halves = ([], [])
        for g in range(GX):
            cos_r, sin_r, cos_i, sin_i = (
                line_ref[2 * g + h, pl.ds(2 * row + p, ROWS, stride=2), :]
                for p in range(2)
                for h in range(2)
            )
            odd_r, odd_i = jnp.where(first, 0.0, sin_r), jnp.where(first, 0.0, sin_i)
            halves[0].append((rounded(cos_r + odd_i), rounded(cos_i - odd_r)))
            even_r, even_i = jnp.where(first, sin_r, cos_r), jnp.where(first, sin_i, cos_i)
            halves[1].append((rounded(even_r - odd_i), rounded(even_i + odd_r)))
        for h, line in enumerate(halves):
            (r0, i0), (r1, i1), (r2, i2), (r3, i3) = line
            even_r, even_i, odd_r, odd_i = r0 + r2, i0 + i2, r1 + r3, i1 + i3
            diff_r, diff_i, turn_r, turn_i = r0 - r2, i0 - i2, i1 - i3, r3 - r1
            formed = (
                (even_r + odd_r, even_i + odd_i),
                (diff_r + turn_r, diff_i + turn_i),
                (even_r - odd_r, even_i - odd_i),
                (diff_r - turn_r, diff_i - turn_i),
            )
            for b, (re, im) in enumerate(formed):
                level_ref[row : row + ROWS, b * GY + h * half : b * GY + (h + 1) * half] = (
                    re * re + im * im
                ).astype(jnp.bfloat16)


def fused_kernel(
    bands,
    samples,
    feed_ref,
    table_ref,
    delay_ref,
    volt_ref,
    out_ref,
    full_ref,
    line_ref,
    level_ref,
    raw_ref,
    lag_out_ref,
    lag_ref,
    select_ref,
    mean_ref,
    total_ref,
    own_ref,
    beam_out_ref,
    beam_in_ref,
    band_out_ref,
    up_ref,
    down_ref,
    raw_sem,
    lag_sems,
    dm_sems,
    beam_sems,
    band_sem,
    up_sem,
    down_sem,
):
    me, column, core = lax.axis_index("freq"), lax.axis_index("beam"), lax.axis_index("dm")
    columns = lax.axis_size("beam")
    channels, feeds = volt_ref.shape[1], volt_ref.shape[4]
    trials = total_ref.shape[1]
    width = feeds // columns
    full_time = 2 * samples
    units = bands * samples
    step = pl.program_id(0)
    other_column, other_core = 1 - column, 1 - core

    def delay_copy(band):
        first = (band * columns + column) * channels
        return pltpu.make_async_copy(
            delay_ref.at[0, pl.ds(first, channels)], raw_ref.at[band], raw_sem.at[band]
        )

    def lag_copy(band):
        shift = lax.rem(band - me + bands, bands)
        return pltpu.make_async_remote_copy(
            src_ref=lag_out_ref.at[band],
            dst_ref=lag_ref.at[me],
            send_sem=lag_sems.at[0, shift],
            recv_sem=lag_sems.at[1, me],
            device_id={"freq": band},
            device_id_type=MESH,
        )

    def lag_arrival(band):
        return pltpu.make_async_remote_copy(
            src_ref=lag_out_ref.at[band],
            dst_ref=lag_ref.at[band],
            send_sem=lag_sems.at[0, 0],
            recv_sem=lag_sems.at[1, band],
            device_id={"freq": band},
            device_id_type=MESH,
        )

    def level_copy(band, sample, owner):
        return pltpu.make_async_remote_copy(
            src_ref=level_ref.at[band, owner * samples + sample],
            dst_ref=level_ref.at[band, owner * samples + sample],
            send_sem=dm_sems.at[0, band * samples + sample],
            recv_sem=dm_sems.at[1, band * samples + sample],
            device_id={"dm": other_core},
            device_id_type=MESH,
        )

    def beam_copy(unit):
        return pltpu.make_async_remote_copy(
            src_ref=beam_out_ref.at[unit],
            dst_ref=beam_in_ref.at[unit],
            send_sem=beam_sems.at[0, unit],
            recv_sem=beam_sems.at[1, unit],
            device_id={"beam": other_column},
            device_id_type=MESH,
        )

    def band_copy(unit, upward):
        return pltpu.make_async_remote_copy(
            src_ref=band_out_ref.at[unit],
            dst_ref=(up_ref if upward else down_ref).at[unit],
            send_sem=band_sem.at[unit],
            recv_sem=(up_sem if upward else down_sem).at[unit],
            device_id={"freq": me + 1 if upward else me - 1},
            device_id_type=MESH,
        )

    @pl.when(step == 0)
    def _():
        for band in range(bands):
            delay_copy(band).start()
        barrier = pltpu.get_barrier_semaphore()
        pl.semaphore_signal(barrier, inc=1, device_id={"dm": other_core}, device_id_type=MESH)
        pl.semaphore_signal(barrier, inc=1, device_id={"beam": other_column}, device_id_type=MESH)
        for shift in range(1, bands):
            pl.semaphore_signal(
                barrier,
                inc=1,
                device_id={"freq": lax.rem(me + shift, bands)},
                device_id_type=MESH,
            )
        for band in range(bands):
            delay_copy(band).wait()
            lag_out_ref[band] = raw_ref[band].astype(jnp.float32).T.astype(jnp.bfloat16)
        pl.semaphore_wait(barrier, bands + 1)
        for band in range(bands):

            @pl.when(band != me)
            def _():
                lag_copy(band).start()

        lag_ref[me] = lag_out_ref[me]
        total_ref[...] = jnp.zeros_like(total_ref)
        place_table(feed_ref, table_ref, full_ref)

    @pl.when(step < units)
    def _():
        band, sample = step // samples, lax.rem(step, samples)
        beamform(volt_ref, full_ref, line_ref, level_ref.at[band, core * samples + sample])
        level_copy(band, sample, core).start()

    @pl.when((step >= samples) & (step < samples + units))
    def _():
        unit = step - samples
        band, row = unit // samples, lax.rem(unit, samples)

        @pl.when(row == 0)
        def _():
            @pl.when(band != me)
            def _():
                lag_arrival(band).wait_recv()

            lag = lag_ref[band].astype(jnp.float32)
            for value in range(LAGS):
                select_ref[:, value * channels : (value + 1) * channels] = jnp.where(
                    lag == value, 1.0, 0.0
                ).astype(jnp.bfloat16)
            for sample in range(samples):
                level_copy(band, sample, other_core).wait_recv()
            share = jnp.full((ROWS, full_time * channels), 1.0 / full_time, jnp.bfloat16)
            for start in range(0, feeds, GY):
                mean_ref[:, start : start + GY] = jnp.dot(
                    share,
                    level_ref[band, :, :, start : start + GY].reshape(full_time * channels, GY),
                    preferred_element_type=jnp.float32,
                )[: mean_ref.shape[0]]

        for start in range(0, feeds, GY):
            cols = slice(start, start + GY)
            levels = level_ref[band, pl.ds(row, LAGS), :, cols].reshape(LAGS * channels, GY)
            summed = jnp.dot(select_ref[...], levels, preferred_element_type=jnp.float32)
            total_ref[row, :, cols] += summed - mean_ref[:1, cols]
        away = pl.multiple_of(other_column * width, width)
        here = pl.multiple_of(column * width, width)
        beam_out_ref[unit] = total_ref[row, :, pl.ds(away, width)].astype(jnp.bfloat16)
        own_ref[unit] = total_ref[row, :, pl.ds(here, width)]
        beam_copy(unit).start()
        level_copy(band, row, core).wait_send()

    @pl.when(step >= samples + BEHIND)
    def _():
        unit = step - samples - BEHIND
        band, row = unit // samples, lax.rem(unit, samples)
        beam_copy(unit).wait()
        own_ref[unit] += beam_in_ref[unit].astype(jnp.float32)

        @pl.when((me > 0) & (me <= band))
        def _():
            band_copy(unit, True).wait_recv()
            own_ref[unit] += up_ref[unit].astype(jnp.float32)

        @pl.when((me < bands - 1) & (me >= band))
        def _():
            band_copy(unit, False).wait_recv()
            own_ref[unit] += down_ref[unit].astype(jnp.float32)

        @pl.when(me != band)
        def _():
            band_out_ref[unit] = own_ref[unit].astype(jnp.bfloat16)

        @pl.when(me < band)
        def _():
            band_copy(unit, True).start()

        @pl.when(me > band)
        def _():
            band_copy(unit, False).start()

        @pl.when(me == band)
        def _():
            half = GY // 2
            lane = lax.broadcasted_iota(jnp.int32, (trials, half), 1)
            back = jnp.where(lane == 0, 0, half - lane)
            factor = 0.125 / math.sqrt(FREQS)
            for start in range(0, width, half):
                part = own_ref[unit, :, start : start + half] * factor
                if start % GY:
                    part = jnp.take_along_axis(part, back, axis=1)
                out_ref[row, :, start : start + half] = part

    @pl.when(step == pl.num_programs(0) - 1)
    def _():
        for band in range(bands):

            @pl.when(band != me)
            def _():
                lag_copy(band).wait_send()

        for unit in range(units):

            @pl.when(unit // samples != me)
            def _():
                band_copy(unit, True).wait_send()


def fused(voltages, grid_feed, delays):
    bands, channels, samples, _, feeds = voltages.shape
    trials = delays.shape[2]
    width = feeds // lax.axis_size("beam")
    units = bands * samples
    vmem, dma = pltpu.VMEM, pltpu.SemaphoreType.DMA

    def block(step):
        step = jnp.minimum(step, units - 1)
        return (step // samples, 0, lax.rem(step, samples), 0, 0)

    return pl.pallas_call(
        functools.partial(fused_kernel, bands, samples),
        grid=(units + samples + BEHIND,),
        in_specs=[
            pl.BlockSpec((1, feeds), lambda i: (0, 0)),
            pl.BlockSpec((GY, GY), lambda i: (0, 0)),
            pl.BlockSpec(memory_space=pl.ANY),
            pl.BlockSpec((1, channels, 1, 2, feeds), block),
        ],
        out_specs=pl.BlockSpec((samples, trials, width), lambda i: (0, 0, 0)),
        out_shape=jax.ShapeDtypeStruct((samples, trials, width), jnp.float32),
        scratch_shapes=[
            vmem((feeds, feeds), jnp.bfloat16),
            vmem((2 * GX, 2 * channels, GY // 2), jnp.float32),
            vmem((bands, 2 * samples, channels, feeds), jnp.bfloat16),
            vmem((bands, channels, trials), jnp.int32),
            vmem((bands, trials, channels), jnp.bfloat16),
            vmem((bands, trials, channels), jnp.bfloat16),
            vmem((trials, LAGS * channels), jnp.bfloat16),
            vmem((8, feeds), jnp.float32),
            vmem((samples, trials, feeds), jnp.float32),
            vmem((units, trials, width), jnp.float32),
            vmem((units, trials, width), jnp.bfloat16),
            vmem((units, trials, width), jnp.bfloat16),
            vmem((units, trials, width), jnp.bfloat16),
            vmem((units, trials, width), jnp.bfloat16),
            vmem((units, trials, width), jnp.bfloat16),
            dma((bands,)),
            dma((2, bands)),
            dma((2, units)),
            dma((2, units)),
            dma((units,)),
            dma((units,)),
            dma((units,)),
        ],
        compiler_params=pltpu.CompilerParams(
            collective_id=0, has_side_effects=True, vmem_limit_bytes=63 * 2**20
        ),
    )(grid_feed.reshape(1, feeds), half_table(), delays, voltages)


def body(voltages, grid_feed, delays):
    bands, channels, samples = voltages.shape[0], voltages.shape[1], voltages.shape[2]
    feeds = voltages.shape[4]
    fits = (
        channels == 256
        and feeds == GX * GY
        and delays.shape[0] == 1
        and delays.shape[2] == 128
        and samples + 1 == LAGS
        and bands == lax.axis_size("freq")
        and lax.axis_size("beam") == 2
        and lax.axis_size("dm") == 2
    )
    if not fits:
        return regrouped_body(voltages, grid_feed, delays)
    return jnp.transpose(fused(voltages, grid_feed, delays), (1, 0, 2))[None]


def solution(mesh):
    in_specs = (P(None, ("freq", "beam"), ("grp", "dm"), None, None), P(), P("freq", None, "dm"))
    out_specs = P("freq", "dm", "grp", "beam")
    return jax.shard_map(body, mesh=mesh, in_specs=in_specs, out_specs=out_specs, check_vma=False)
```

profile of v0, /device:TPU:24, one launch (start us, length us, event | category | flops | bytes accessed | tf_op | source)
XLA Modules:
  0.0 99.7 jit_solution(5100444758660064186)
XLA Ops:
  0.0 96.8 %shard_map.46 = f32[4,128,512]{2,1,0:T(8,128)} custom-call(s32[1,1024]{1,0:T(1,128)} %bitcast.5, bf16[256,256]{1,0:T(8,128)(2,1)} %constant.2.clone.table_ref, s32[1,2048,128]{2,1,0:T(8,128)} %delay_ref.1, bf16[4,256,4,2,1024]{4,3,2,1,0:T(2,128)(2,1)} %volt_ref.1), custom_call_target="tpu_custom_call" | custom-call | tf_op jit(solution)/shard_map/pallas_call | solution.py:411
  96.8 2.9 %copy.5 = f32[1,128,4,512]{3,2,1,0:T(4,128)} copy(f32[1,128,4,512]{3,1,2,0:T(8,128)} %bitcast.4) | data formatting | bytes 2097152 | tf_op jit(solution)/shard_map/broadcast_in_dim | solution.py:467
where the time goes:
time: 99.9 us; the launch traced here: 99.7 us
  Pallas kernels  96.8 us (97%)
  local copies, waits for them, and re-layouts  2.87 us (3%)
    pallas_call x1, Pallas kernels, fused(): pl.pallas_call(functools.partial(fused_kernel, bands, samples), grid=(uni...  96.8 us
    broadcast_in_dim x1, local copies, waits for them, and re-layouts, body(): return jnp.transpose(fused(voltages, grid_feed, delays), (1, 0, 2))[None]  2.87 us

commit v1 on v0

--- a/solution.py
+++ b/solution.py
@@ -14,7 +14,9 @@
 FREQS = 8192
 ROWS = 16
 LAGS = 5
-BEHIND = 5
+HOP = 2
+SLOTS = 4
+PIECES = 2
 MESH = pl.DeviceIdType.MESH
 
 
@@ -121,54 +123,64 @@
 def place_table(feed_ref, table_ref, full_ref):
     feeds = full_ref.shape[0]
     feed = lax.broadcasted_iota(jnp.int32, (feeds, GY), 0)
-    for g in range(GX):
-        cells = slice(g * GY, (g + 1) * GY)
+
+    @pl.loop(0, GX)
+    def _(g):
+        cells = pl.ds(pl.multiple_of(g * GY, GY), GY)
         placed = jnp.where(feed == feed_ref[:, cells], 1.0, 0.0).astype(jnp.bfloat16)
         full_ref[:, cells] = jnp.dot(
             placed, table_ref[...], preferred_element_type=jnp.float32
         ).astype(jnp.bfloat16)
 
 
-def beamform(volt_ref, full_ref, line_ref, level_ref):
-    channels, feeds = volt_ref.shape[1], volt_ref.shape[4]
+def transform_y(pairs_ref, full_ref, line_ref, g):
+    channels, _, feeds = pairs_ref.shape
+    line = jnp.dot(
+        pairs_ref[...].reshape(2 * channels, feeds),
+        full_ref[:, g * GY : (g + 1) * GY],
+        preferred_element_type=jnp.float32,
+    )
+    line_ref[2 * g], line_ref[2 * g + 1] = line[:, : GY // 2], line[:, GY // 2 :]
+
+
+def transform_x(line_ref, level_ref, row):
     half = GY // 2
-    pairs = volt_ref[0, :, 0].reshape(2 * channels, feeds)
-    for g in range(GX):
-        line = jnp.dot(
-            pairs, full_ref[:, g * GY : (g + 1) * GY], preferred_element_type=jnp.float32
-        )
-        line_ref[2 * g], line_ref[2 * g + 1] = line[:, :half], line[:, half:]
     first = lax.broadcasted_iota(jnp.int32, (ROWS, half), 1) == 0
 
     def rounded(a):
         return a.astype(jnp.bfloat16).astype(jnp.float32)
 
-    for row in range(0, channels, ROWS):
-        halves = ([], [])
-        for g in range(GX):
-            cos_r, sin_r, cos_i, sin_i = (
-                line_ref[2 * g + h, pl.ds(2 * row + p, ROWS, stride=2), :]
-                for p in range(2)
-                for h in range(2)
-            )
-            odd_r, odd_i = jnp.where(first, 0.0, sin_r), jnp.where(first, 0.0, sin_i)
-            halves[0].append((rounded(cos_r + odd_i), rounded(cos_i - odd_r)))
-            even_r, even_i = jnp.where(first, sin_r, cos_r), jnp.where(first, sin_i, cos_i)
-            halves[1].append((rounded(even_r - odd_i), rounded(even_i + odd_r)))
-        for h, line in enumerate(halves):
-            (r0, i0), (r1, i1), (r2, i2), (r3, i3) = line
-            even_r, even_i, odd_r, odd_i = r0 + r2, i0 + i2, r1 + r3, i1 + i3
-            diff_r, diff_i, turn_r, turn_i = r0 - r2, i0 - i2, i1 - i3, r3 - r1
-            formed = (
-                (even_r + odd_r, even_i + odd_i),
-                (diff_r + turn_r, diff_i + turn_i),
-                (even_r - odd_r, even_i - odd_i),
-                (diff_r - turn_r, diff_i - turn_i),
-            )
-            for b, (re, im) in enumerate(formed):
-                level_ref[row : row + ROWS, b * GY + h * half : b * GY + (h + 1) * half] = (
-                    re * re + im * im
-                ).astype(jnp.bfloat16)
+    halves = ([], [])
+    for g in range(GX):
+        cos_r, sin_r, cos_i, sin_i = (
+            line_ref[2 * g + h, pl.ds(2 * row + p, ROWS, stride=2), :]
+            for p in range(2)
+            for h in range(2)
+        )
+        odd_r, odd_i = jnp.where(first, 0.0, sin_r), jnp.where(first, 0.0, sin_i)
+        halves[0].append((rounded(cos_r + odd_i), rounded(cos_i - odd_r)))
+        even_r, even_i = jnp.where(first, sin_r, cos_r), jnp.where(first, sin_i, cos_i)
+        halves[1].append((rounded(even_r - odd_i), rounded(even_i + odd_r)))
+    for h, line in enumerate(halves):
+        (r0, i0), (r1, i1), (r2, i2), (r3, i3) = line
+        even_r, even_i, odd_r, odd_i = r0 + r2, i0 + i2, r1 + r3, i1 + i3
+        diff_r, diff_i, turn_r, turn_i = r0 - r2, i0 - i2, i1 - i3, r3 - r1
+        formed = (
+            (even_r + odd_r, even_i + odd_i),
+            (diff_r + turn_r, diff_i + turn_i),
+            (even_r - odd_r, even_i - odd_i),
+            (diff_r - turn_r, diff_i - turn_i),
+        )
+        for b, (re, im) in enumerate(formed):
+            level_ref[row : row + ROWS, b * GY + h * half : b * GY + (h + 1) * half] = (
+                re * re + im * im
+            ).astype(jnp.bfloat16)
+
+
+def send_order(bands, samples):
+    units = [(0, 0), (1, 0), (1, 1), (1, 2), (0, 1), (2, 0), (2, 1), (0, 2), (0, 3)]
+    units += [(3, row) for row in range(samples)] + [(2, 2), (2, 3), (1, 3)]
+    return [band * samples + row for band, row in units]
 
 
 def fused_kernel(
@@ -180,7 +192,9 @@
     volt_ref,
     out_ref,
     full_ref,
-    line_ref,
+    held_ref,
+    line0_ref,
+    line1_ref,
     level_ref,
     raw_ref,
     lag_out_ref,
@@ -194,6 +208,7 @@
     band_out_ref,
     up_ref,
     down_ref,
+    volt_sem,
     raw_sem,
     lag_sems,
     dm_sems,
@@ -205,12 +220,23 @@
     me, column, core = lax.axis_index("freq"), lax.axis_index("beam"), lax.axis_index("dm")
     columns = lax.axis_size("beam")
     channels, feeds = volt_ref.shape[1], volt_ref.shape[4]
+    slots, part = held_ref.shape[0], channels // 2
     trials = total_ref.shape[1]
     width = feeds // columns
     full_time = 2 * samples
     units = bands * samples
-    step = pl.program_id(0)
     other_column, other_core = 1 - column, 1 - core
+
+    def rows_of(piece):
+        return slice(piece * trials // PIECES, (piece + 1) * trials // PIECES)
+
+    order = send_order(bands, samples)
+
+    def unit_at(place):
+        found = jnp.int32(order[0])
+        for at, unit in enumerate(order[1:]):
+            found = jnp.where(place > at, unit, found)
+        return found
 
     def delay_copy(band):
         first = (band * columns + column) * channels
@@ -249,30 +275,37 @@
             device_id_type=MESH,
         )
 
-    def beam_copy(unit):
+    def beam_copy(unit, piece):
         return pltpu.make_async_remote_copy(
-            src_ref=beam_out_ref.at[unit],
-            dst_ref=beam_in_ref.at[unit],
-            send_sem=beam_sems.at[0, unit],
-            recv_sem=beam_sems.at[1, unit],
+            src_ref=beam_out_ref.at[unit, rows_of(piece)],
+            dst_ref=beam_in_ref.at[unit, rows_of(piece)],
+            send_sem=beam_sems.at[0, unit * PIECES + piece],
+            recv_sem=beam_sems.at[1, unit * PIECES + piece],
             device_id={"beam": other_column},
             device_id_type=MESH,
         )
 
-    def band_copy(unit, upward):
+    def band_copy(unit, piece, upward):
         return pltpu.make_async_remote_copy(
-            src_ref=band_out_ref.at[unit],
-            dst_ref=(up_ref if upward else down_ref).at[unit],
-            send_sem=band_sem.at[unit],
-            recv_sem=(up_sem if upward else down_sem).at[unit],
+            src_ref=band_out_ref.at[unit, rows_of(piece)],
+            dst_ref=(up_ref if upward else down_ref).at[unit, rows_of(piece)],
+            send_sem=band_sem.at[unit * PIECES + piece],
+            recv_sem=(up_sem if upward else down_sem).at[unit * PIECES + piece],
             device_id={"freq": me + 1 if upward else me - 1},
             device_id_type=MESH,
         )
 
-    @pl.when(step == 0)
-    def _():
+    def volt_copy(step):
+        band, sample, slot = step // samples, lax.rem(step, samples), lax.rem(step, slots)
+        return pltpu.make_async_copy(
+            volt_ref.at[band, :, sample], held_ref.at[slot], volt_sem.at[slot]
+        )
+
+    def enter():
         for band in range(bands):
             delay_copy(band).start()
+        for step in range(slots - 1):
+            volt_copy(step).start()
         barrier = pltpu.get_barrier_semaphore()
         pl.semaphore_signal(barrier, inc=1, device_id={"dm": other_core}, device_id_type=MESH)
         pl.semaphore_signal(barrier, inc=1, device_id={"beam": other_column}, device_id_type=MESH)
@@ -283,11 +316,15 @@
                 device_id={"freq": lax.rem(me + shift, bands)},
                 device_id_type=MESH,
             )
-        for band in range(bands):
+        place_table(feed_ref, table_ref, full_ref)
+
+    def share_lags():
+        @pl.loop(0, bands)
+        def _(band):
             delay_copy(band).wait()
             lag_out_ref[band] = raw_ref[band].astype(jnp.float32).T.astype(jnp.bfloat16)
-        pl.semaphore_wait(barrier, bands + 1)
-        for band in range(bands):
+        pl.semaphore_wait(pltpu.get_barrier_semaphore(), bands + 1)
+        for band in reversed(range(bands)):
 
             @pl.when(band != me)
             def _():
@@ -295,42 +332,57 @@
 
         lag_ref[me] = lag_out_ref[me]
         total_ref[...] = jnp.zeros_like(total_ref)
-        place_table(feed_ref, table_ref, full_ref)
-
-    @pl.when(step < units)
-    def _():
+
+    def form_beams(step):
         band, sample = step // samples, lax.rem(step, samples)
-        beamform(volt_ref, full_ref, line_ref, level_ref.at[band, core * samples + sample])
+        levels_ref = level_ref.at[band, core * samples + sample]
+        volt_copy(step).wait()
+
+        @pl.when(step + slots - 1 < units)
+        def _():
+            volt_copy(step + slots - 1).start()
+
+        block_ref = held_ref.at[lax.rem(step, slots)]
+        rows = range(0, part, ROWS)
+        for g in range(GX):
+            transform_y(block_ref.at[:part], full_ref, line0_ref, g)
+        for g in range(GX):
+            transform_y(block_ref.at[part:], full_ref, line1_ref, g)
+            for row in rows[g::GX]:
+                transform_x(line0_ref, levels_ref.at[:part], row)
+        for row in rows:
+            transform_x(line1_ref, levels_ref.at[part:], row)
+
+        @pl.when(step == 0)
+        def _():
+            share_lags()
+
         level_copy(band, sample, core).start()
 
-    @pl.when((step >= samples) & (step < samples + units))
-    def _():
-        unit = step - samples
+    def prepare(band):
+        @pl.when(band != me)
+        def _():
+            lag_arrival(band).wait_recv()
+
+        lag = lag_ref[band].astype(jnp.float32)
+        for value in range(LAGS):
+            select_ref[:, value * channels : (value + 1) * channels] = jnp.where(
+                lag == value, 1.0, 0.0
+            ).astype(jnp.bfloat16)
+        for sample in range(samples):
+            level_copy(band, sample, other_core).wait_recv()
+        share = jnp.full((ROWS, full_time * channels), 1.0 / full_time, jnp.bfloat16)
+        for start in range(0, feeds, GY):
+            mean_ref[:, start : start + GY] = jnp.dot(
+                share,
+                level_ref[band, :, :, start : start + GY].reshape(full_time * channels, GY),
+                preferred_element_type=jnp.float32,
+            )[: mean_ref.shape[0]]
+
+    def sum_channels(unit):
         band, row = unit // samples, lax.rem(unit, samples)
-
-        @pl.when(row == 0)
-        def _():
-            @pl.when(band != me)
-            def _():
-                lag_arrival(band).wait_recv()
-
-            lag = lag_ref[band].astype(jnp.float32)
-            for value in range(LAGS):
-                select_ref[:, value * channels : (value + 1) * channels] = jnp.where(
-                    lag == value, 1.0, 0.0
-                ).astype(jnp.bfloat16)
-            for sample in range(samples):
-                level_copy(band, sample, other_core).wait_recv()
-            share = jnp.full((ROWS, full_time * channels), 1.0 / full_time, jnp.bfloat16)
-            for start in range(0, feeds, GY):
-                mean_ref[:, start : start + GY] = jnp.dot(
-                    share,
-                    level_ref[band, :, :, start : start + GY].reshape(full_time * channels, GY),
-                    preferred_element_type=jnp.float32,
-                )[: mean_ref.shape[0]]
-
-        for start in range(0, feeds, GY):
-            cols = slice(start, start + GY)
+        for g in range(GX):
+            cols = slice(g * GY, (g + 1) * GY)
             levels = level_ref[band, pl.ds(row, LAGS), :, cols].reshape(LAGS * channels, GY)
             summed = jnp.dot(select_ref[...], levels, preferred_element_type=jnp.float32)
             total_ref[row, :, cols] += summed - mean_ref[:1, cols]
@@ -338,63 +390,141 @@
         here = pl.multiple_of(column * width, width)
         beam_out_ref[unit] = total_ref[row, :, pl.ds(away, width)].astype(jnp.bfloat16)
         own_ref[unit] = total_ref[row, :, pl.ds(here, width)]
-        beam_copy(unit).start()
         level_copy(band, row, core).wait_send()
 
-    @pl.when(step >= samples + BEHIND)
-    def _():
-        unit = step - samples - BEHIND
-        band, row = unit // samples, lax.rem(unit, samples)
-        beam_copy(unit).wait()
-        own_ref[unit] += beam_in_ref[unit].astype(jnp.float32)
-
-        @pl.when((me > 0) & (me <= band))
+    def send_sums(unit):
+        for piece in range(PIECES):
+            beam_copy(unit, piece).start()
+
+    def forward(unit, piece, upward):
+        rows = rows_of(piece)
+        band_out_ref[unit, rows] = own_ref[unit, rows].astype(jnp.bfloat16)
+        band_copy(unit, piece, upward).start()
+
+    def arrive(unit, piece, upward):
+        rows = rows_of(piece)
+        band_copy(unit, piece, upward).wait_recv()
+        own_ref[unit, rows] += (up_ref if upward else down_ref)[unit, rows].astype(jnp.float32)
+
+    def links(place):
+        @pl.when(place < units)
         def _():
-            band_copy(unit, True).wait_recv()
-            own_ref[unit] += up_ref[unit].astype(jnp.float32)
-
-        @pl.when((me < bands - 1) & (me >= band))
-        def _():
-            band_copy(unit, False).wait_recv()
-            own_ref[unit] += down_ref[unit].astype(jnp.float32)
-
-        @pl.when(me != band)
-        def _():
-            band_out_ref[unit] = own_ref[unit].astype(jnp.bfloat16)
-
-        @pl.when(me < band)
-        def _():
-            band_copy(unit, True).start()
-
-        @pl.when(me > band)
-        def _():
-            band_copy(unit, False).start()
-
-        @pl.when(me == band)
-        def _():
-            half = GY // 2
-            lane = lax.broadcasted_iota(jnp.int32, (trials, half), 1)
-            back = jnp.where(lane == 0, 0, half - lane)
-            factor = 0.125 / math.sqrt(FREQS)
+            unit = unit_at(place)
+            band = unit // samples
+            for piece in range(PIECES):
+                rows = rows_of(piece)
+                beam_copy(unit, piece).wait()
+                own_ref[unit, rows] += beam_in_ref[unit, rows].astype(jnp.float32)
+
+                @pl.when((me == 0) & (band > 0))
+                def _():
+                    forward(unit, piece, True)
+
+                @pl.when((me == bands - 1) & (band < me))
+                def _():
+                    forward(unit, piece, False)
+
+        for upward in (True, False):
+            hop = me if upward else bands - 1 - me
+            earlier = place - HOP * hop
+            unit = unit_at(jnp.maximum(earlier, 0))
+            band = unit // samples
+            beyond = band > me if upward else band < me
+
+            @pl.when((hop > 0) & (earlier >= 0) & (earlier < units) & beyond)
+            def _():
+                for piece in range(PIECES):
+                    arrive(unit, piece, upward)
+                    forward(unit, piece, upward)
+
+    def leave():
+        half = GY // 2
+        lane = lax.broadcasted_iota(jnp.int32, (trials, half), 1)
+        back = jnp.where(lane == 0, 0, half - lane)
+        factor = 0.125 / math.sqrt(FREQS)
+
+        @pl.loop(0, samples)
+        def _(row):
+            unit = me * samples + row
+
+            for piece in range(PIECES):
+
+                @pl.when(me > 0)
+                def _():
+                    arrive(unit, piece, True)
+
+                @pl.when(me < bands - 1)
+                def _():
+                    arrive(unit, piece, False)
+
             for start in range(0, width, half):
                 part = own_ref[unit, :, start : start + half] * factor
                 if start % GY:
                     part = jnp.take_along_axis(part, back, axis=1)
                 out_ref[row, :, start : start + half] = part
 
-    @pl.when(step == pl.num_programs(0) - 1)
-    def _():
         for band in range(bands):
 
             @pl.when(band != me)
             def _():
                 lag_copy(band).wait_send()
 
-        for unit in range(units):
-
+        @pl.loop(0, units)
+        def _(unit):
             @pl.when(unit // samples != me)
             def _():
-                band_copy(unit, True).wait_send()
+                for piece in range(PIECES):
+                    band_copy(unit, piece, True).wait_send()
+
+    def form_band(band, place):
+        @pl.loop(0, samples)
+        def _(sample):
+            form_beams(band * samples + sample)
+            if place is not None:
+
+                @pl.when(lax.rem(sample, 2) == 1)
+                def _():
+                    links(place + sample // 2)
+
+    def sum_band(band, at_once):
+        prepare(band)
+
+        @pl.loop(0, samples)
+        def _(row):
+            sum_channels(band * samples + row)
+
+            @pl.when(row < at_once)
+            def _():
+                send_sums(band * samples + row)
+
+    def send_at(first, last):
+        for unit in order[first:last]:
+            send_sums(unit)
+
+    enter()
+
+    @pl.loop(0, 2 * samples)
+    def _(step):
+        form_beams(step)
+
+    sum_band(0, 1)
+    sum_band(1, 3)
+    send_at(4, 5)
+    links(0)
+    form_band(2, 1)
+    sum_band(2, 2)
+    send_at(7, 9)
+    links(3)
+    form_band(3, 4)
+    sum_band(3, samples)
+    send_at(9 + samples, units)
+    links(6)
+
+    @pl.loop(7, units + HOP * (bands - 2))
+    def _(place):
+        links(place)
+
+    leave()
 
 
 def fused(voltages, grid_feed, delays):
@@ -404,24 +534,21 @@
     units = bands * samples
     vmem, dma = pltpu.VMEM, pltpu.SemaphoreType.DMA
 
-    def block(step):
-        step = jnp.minimum(step, units - 1)
-        return (step // samples, 0, lax.rem(step, samples), 0, 0)
-
     return pl.pallas_call(
         functools.partial(fused_kernel, bands, samples),
-        grid=(units + samples + BEHIND,),
         in_specs=[
-            pl.BlockSpec((1, feeds), lambda i: (0, 0)),
-            pl.BlockSpec((GY, GY), lambda i: (0, 0)),
+            pl.BlockSpec(memory_space=vmem),
+            pl.BlockSpec(memory_space=vmem),
             pl.BlockSpec(memory_space=pl.ANY),
-            pl.BlockSpec((1, channels, 1, 2, feeds), block),
+            pl.BlockSpec(memory_space=pl.ANY),
         ],
-        out_specs=pl.BlockSpec((samples, trials, width), lambda i: (0, 0, 0)),
+        out_specs=pl.BlockSpec(memory_space=vmem),
         out_shape=jax.ShapeDtypeStruct((samples, trials, width), jnp.float32),
         scratch_shapes=[
             vmem((feeds, feeds), jnp.bfloat16),
-            vmem((2 * GX, 2 * channels, GY // 2), jnp.float32),
+            vmem((SLOTS, channels, 2, feeds), jnp.bfloat16),
+            vmem((2 * GX, channels, GY // 2), jnp.float32),
+            vmem((2 * GX, channels, GY // 2), jnp.float32),
             vmem((bands, 2 * samples, channels, feeds), jnp.bfloat16),
             vmem((bands, channels, trials), jnp.int32),
             vmem((bands, trials, channels), jnp.bfloat16),
@@ -435,13 +562,14 @@
             vmem((units, trials, width), jnp.bfloat16),
             vmem((units, trials, width), jnp.bfloat16),
             vmem((units, trials, width), jnp.bfloat16),
+            dma((SLOTS,)),
             dma((bands,)),
             dma((2, bands)),
             dma((2, units)),
-            dma((2, units)),
-            dma((units,)),
-            dma((units,)),
-            dma((units,)),
+            dma((2, units * PIECES)),
+            dma((units * PIECES,)),
+            dma((units * PIECES,)),
+            dma((units * PIECES,)),
         ],
         compiler_params=pltpu.CompilerParams(
             collective_id=0, has_side_effects=True, vmem_limit_bytes=63 * 2**20
@@ -458,6 +586,7 @@
         and delays.shape[0] == 1
         and delays.shape[2] == 128
         and samples + 1 == LAGS
+        and bands == 4
         and bands == lax.axis_size("freq")
         and lax.axis_size("beam") == 2
         and lax.axis_size("dm") == 2

time: 99.9 us -> 80.6 us (0.81)
  Pallas kernels: 96.8 us -> 76.5 us
    pallas_call x1, Pallas kernels: 96.8 us -> 76.5 us  [fused(): pl.pallas_call(functools.partial(fused_kernel, bands, samples), in_specs=...]
where the time goes in v1:
time: 80.6 us; the launch traced here: 79.4 us
  Pallas kernels  76.5 us (95%)
  local copies, waits for them, and re-layouts  2.87 us (4%)
    pallas_call x1, Pallas kernels, fused(): pl.pallas_call(functools.partial(fused_kernel, bands, samples), in_specs=...  76.5 us
    broadcast_in_dim x1, local copies, waits for them, and re-layouts, body(): return jnp.transpose(fused(voltages, grid_feed, delays), (1, 0, 2))[None]  2.87 us

profile of v1, /device:TPU:24, one launch (start us, length us, event | category | flops | bytes accessed | tf_op | source)
XLA Modules:
  0.0 79.4 jit_solution(14349824890475691491)
XLA Ops:
  0.0 76.5 %shard_map.46 = f32[4,128,512]{2,1,0:T(8,128)} custom-call(s32[1,1024]{1,0:T(1,128)} %bitcast.5, bf16[256,256]{1,0:T(8,128)(2,1)} %constant.2.clone.table_ref, s32[1,2048,128]{2,1,0:T(8,128)} %delay_ref.1, bf16[4,256,4,2,1024]{4,3,2,1,0:T(2,128)(2,1)} %volt_ref.1), custom_call_target="tpu_custom_call" | custom-call | tf_op jit(solution)/shard_map/pallas_call | solution.py:537
  76.6 2.9 %copy.5 = f32[1,128,4,512]{3,2,1,0:T(4,128)} copy(f32[1,128,4,512]{3,1,2,0:T(8,128)} %bitcast.4) | data formatting | bytes 2097152 | tf_op jit(solution)/shard_map/broadcast_in_dim | solution.py:596

commit v2 on v1

--- a/solution.py
+++ b/solution.py
@@ -443,8 +443,7 @@
         back = jnp.where(lane == 0, 0, half - lane)
         factor = 0.125 / math.sqrt(FREQS)
 
-        @pl.loop(0, samples)
-        def _(row):
+        for row in range(samples):
             unit = me * samples + row
 
             for piece in range(PIECES):
@@ -461,7 +460,7 @@
                 part = own_ref[unit, :, start : start + half] * factor
                 if start % GY:
                     part = jnp.take_along_axis(part, back, axis=1)
-                out_ref[row, :, start : start + half] = part
+                out_ref[:, row, start : start + half] = part
 
         for band in range(bands):
 
@@ -543,7 +542,7 @@
             pl.BlockSpec(memory_space=pl.ANY),
         ],
         out_specs=pl.BlockSpec(memory_space=vmem),
-        out_shape=jax.ShapeDtypeStruct((samples, trials, width), jnp.float32),
+        out_shape=jax.ShapeDtypeStruct((trials, samples, width), jnp.float32),
         scratch_shapes=[
             vmem((feeds, feeds), jnp.bfloat16),
             vmem((SLOTS, channels, 2, feeds), jnp.bfloat16),
@@ -593,7 +592,7 @@
     )
     if not fits:
         return regrouped_body(voltages, grid_feed, delays)
-    return jnp.transpose(fused(voltages, grid_feed, delays), (1, 0, 2))[None]
+    return fused(voltages, grid_feed, delays)[None]
 
 
 def solution(mesh):

time: 80.6 us -> 80.1 us (level)
    broadcast_in_dim x1 -> x0, local copies, waits for them, and re-layouts: 2.87 us -> none  [body(): return jnp.transpose(fused(voltages, grid_feed, delays), (1, 0, 2))[None]]
    unnamed x0 -> x1, local copies, waits for them, and re-layouts: none -> 2.26 us
where the time goes in v2:
time: 80.1 us; the launch traced here: 78.9 us
  Pallas kernels  76.7 us (96%)
  local copies, waits for them, and re-layouts  2.26 us (3%)
    pallas_call x1, Pallas kernels, fused(): pl.pallas_call(functools.partial(fused_kernel, bands, samples), in_specs=...  76.7 us
    unnamed x1, local copies, waits for them, and re-layouts  2.26 us

profile of v2, /device:TPU:24, one launch (start us, length us, event | category | flops | bytes accessed | tf_op | source)
XLA Modules:
  0.0 78.9 jit_solution(12993930240918991344)
XLA Ops:
  0.0 76.7 %shard_map.46 = f32[128,4,512]{2,1,0:T(4,128)} custom-call(s32[1,1024]{1,0:T(1,128)} %bitcast.3, bf16[256,256]{1,0:T(8,128)(2,1)} %constant.2.clone.table_ref, s32[1,2048,128]{2,1,0:T(8,128)} %delay_ref.1, bf16[4,256,4,2,1024]{4,3,2,1,0:T(2,128)(2,1)} %volt_ref.1), custom_call_target="tpu_custom_call" | custom-call | tf_op jit(solution)/shard_map/pallas_call | solution.py:536
  76.7 2.3 %copy.6 = f32[1,128,4,512]{3,2,1,0:T(4,128)} copy(f32[1,128,4,512]{3,2,1,0:T(4,128)} %bitcast.2) | data formatting | bytes 2097152
